TPU v7x, 32 devices: a whole 2x2x4 slice. The times are simulated.
32 devices in a mesh: groups: 2 (over x), row: 8 (over z, y), head: 2 (over core).
Axes of the slice: x: 2, y: 2, z: 4, core: 2. Of those that a mesh axis runs over, the one named last changes fastest.
Arguments:
- hidden: bfloat16 [48, 4096], P('groups'), parts along dimension 0, may hold values from -6 to 6
- norm_gain: float32 [4096], replicated, may hold values from 0.1 to 1.9
- w_query: bfloat16 [8, 256, 4096], P('head', 'row'), may hold values from -0.09375 to 0.09375
- w_key: bfloat16 [8, 256, 4096], P('head', 'row'), may hold values from -0.09375 to 0.09375
- w_value: bfloat16 [8, 512, 4096], P('head', 'row'), may hold values from -0.09375 to 0.09375
- w_outgate: bfloat16 [8, 512, 4096], P('head', 'row'), may hold values from -0.09375 to 0.09375
- w_out: bfloat16 [8, 512, 4096], P('head', 'row'), may hold values from -0.125 to 0.125
- w_gates: bfloat16 [2, 8, 4096], P(None, 'head'), may hold values from -0.09375 to 0.09375
- gate_bias: float32 [2, 8], P(None, 'head'), may hold values from -2 to 4
- headnorm_gain: float32 [8, 512], P('head', 'row'), may hold values from 0.1 to 1.9
- final_gain: float32 [4096], replicated, may hold values from 0.1 to 1.9
- w_vocab: bfloat16 [25152, 4096], P(('row', 'head')), may hold values from -39.0625 to 39.0625
- memory: float32 [48, 8, 256, 512], P('groups', 'head', 'row'), parts along dimension 0, may hold values from -6 to 6
- normalizer: float32 [48, 8, 256], P('groups', 'head', 'row'), parts along dimension 0, may hold values from -6 to 6
- stabilizer: float32 [48, 8], P('groups', 'head'), parts along dimension 0, may hold values from -2 to 2
- targets: int32 [48], P('groups'), parts along dimension 0, may hold values from 0 to 25151
Outputs:
- memory_out: float32 [48, 8, 256, 512], P('groups', 'head', 'row'), parts along dimension 0
- normalizer_out: float32 [48, 8, 256], P('groups', 'head', 'row'), parts along dimension 0
- stabilizer_out: float32 [48, 8], P('groups', 'head'), parts along dimension 0
- hidden_out: bfloat16 [48, 4096], P('groups', ('row', 'head')), parts along dimension 0
- log_prob: float32 [48], P('groups'), parts along dimension 0
There are 2 independent parts, one for each index of `groups`. A program takes and returns all parts, laid end to end along the dimension named above; an argument that names none is the same for every part. Nothing has to cross between parts.
All inputs are finite; a program needn't handle non-finite values.
Results may differ from a plain program's by a relative error of at most 0.0035.
The roundings to bfloat16 on the way count: a program that leaves them out, or rounds other values in their place, can miss the bound.
Values may be sent and summed in bfloat16 or wider, within the bound.
A program may use at most 64 MiB of HBM per device.

v0:
```python
import math
import jax
import jax.numpy as jnp
from jax import lax
from jax.sharding import PartitionSpec as P

QK_DIM = 256
epsilon = 1e-06


def joined_2(value, axis, join):
    pieces = jax.tree.map(lambda part: lax.all_gather(part, axis), value)
    head = jax.tree.map(lambda part: part[0], pieces)
    tail = jax.tree.map(lambda part: part[1:], pieces)
    total, _ = lax.scan(lambda total, share: (join(total, share), None), head, tail)
    return total


def rms_round(stream, gain):
    scale = lax.rsqrt(jnp.mean(stream * stream, axis=-1, keepdims=True) + epsilon)
    return (stream * scale * gain).astype(jnp.bfloat16)


def per_device(
    hidden,
    norm_gain,
    w_query,
    w_key,
    w_value,
    w_outgate,
    w_out,
    w_gates,
    gate_bias,
    headnorm_gain,
    final_gain,
    w_vocab,
    memory,
    normalizer,
    stabilizer,
    targets,
):
    value_rows = w_value.shape[1]
    stream = hidden.astype(jnp.float32)
    normed_in = rms_round(stream, norm_gain)

    def project(weights):
        return jnp.einsum("sd,hjd->shj", normed_in, weights, preferred_element_type=jnp.float32)

    queries = project(w_query) / math.sqrt(QK_DIM)
    key_part = project(w_key)
    value_part = project(w_value).astype(jnp.bfloat16)
    outgate_pre = project(w_outgate)
    gate_pre = (
        jnp.einsum("sd,ghd->gsh", normed_in, w_gates, preferred_element_type=jnp.float32)
        + gate_bias[:, None, :]
    )
    log_forget = jax.nn.log_sigmoid(gate_pre[1])
    stabilizer_out = jnp.maximum(log_forget + stabilizer, gate_pre[0])
    decay_rate = jnp.exp(log_forget + stabilizer - stabilizer_out)
    inflow = jnp.exp(gate_pre[0] - stabilizer_out)
    scaled_key = inflow[:, :, None] * key_part
    memory_out = (
        decay_rate[:, :, None, None] * memory
        + scaled_key[:, :, :, None]
        * lax.all_gather(value_part, "row", axis=2, tiled=True).astype(jnp.float32)[:, :, None, :]
    )
    normalizer_out = decay_rate[:, :, None] * normalizer + scaled_key
    partial_readout = jnp.einsum(
        "shj,shje->she", queries, memory_out, precision=lax.Precision.HIGHEST
    )
    readout = lax.psum(partial_readout, "row")
    average = jnp.mean(readout, axis=-1)
    centered_full = readout - average[:, :, None]
    variance = jnp.mean(centered_full * centered_full, axis=-1)
    centered = lax.dynamic_slice_in_dim(
        centered_full, lax.axis_index("row") * value_rows, value_rows, 2
    )
    normed = centered * lax.rsqrt(variance + epsilon)[:, :, None] * headnorm_gain
    gated_out = (jax.nn.sigmoid(outgate_pre) * normed).astype(jnp.bfloat16)
    partial_terms = jnp.einsum("shj,hjd->sd", gated_out, w_out, preferred_element_type=jnp.float32)
    position = lax.axis_index("row") * lax.axis_size("head") + lax.axis_index("head")
    share_width = hidden.shape[1] // (lax.axis_size("row") * lax.axis_size("head"))
    vocab_here = w_vocab.shape[0]
    projection = lax.psum(partial_terms, ("row", "head"))
    new_full = (stream + projection).astype(jnp.bfloat16)
    final_feat = rms_round(new_full.astype(jnp.float32), final_gain)
    logits = jnp.einsum("sd,vd->sv", final_feat, w_vocab, preferred_element_type=jnp.float32)
    hidden_out = lax.dynamic_slice_in_dim(new_full, position * share_width, share_width, 1)
    local_ids = targets - position * vocab_here
    is_target = jnp.arange(vocab_here, dtype=jnp.int32)[None, :] == local_ids[:, None]
    target_term = jnp.sum(jnp.where(is_target, logits, 0.0), axis=-1)
    local_max = jnp.max(logits, axis=-1)
    local_sum = jnp.sum(jnp.exp(logits - local_max[:, None]), axis=-1)

    def combine(earlier, later):
        highest = jnp.maximum(earlier[0], later[0])
        joined = earlier[1] * jnp.exp(earlier[0] - highest) + later[1] * jnp.exp(later[0] - highest)
        return (highest, joined, earlier[2] + later[2])

    highest, exp_total, picked = joined_2(
        (local_max, local_sum, target_term), ("row", "head"), combine
    )
    log_prob = picked - (highest + jnp.log(exp_total))
    return (memory_out, normalizer_out, stabilizer_out, hidden_out, log_prob)


def solution(mesh):
    in_specs = (
        P("groups", None),
        P(),
        P("head", "row", None),
        P("head", "row", None),
        P("head", "row", None),
        P("head", "row", None),
        P("head", "row", None),
        P(None, "head", None),
        P(None, "head"),
        P("head", "row"),
        P(),
        P(("row", "head"), None),
        P("groups", "head", "row", None),
        P("groups", "head", "row"),
        P("groups", "head"),
        P("groups"),
    )
    out_specs = (
        P("groups", "head", "row", None),
        P("groups", "head", "row"),
        P("groups", "head"),
        P("groups", ("row", "head")),
        P("groups"),
    )
    return jax.shard_map(
        per_device, mesh=mesh, in_specs=in_specs, out_specs=out_specs, check_vma=False
    )
```

profile of v0, /device:TPU:0, one launch (start us, length us, event | category | flops | bytes accessed | tf_op | source)
XLA Modules:
  0.0 280.0 jit_solution(1592682969917463788)
XLA Ops:
  7.2 1.2 fusion.17
  8.5 2.7 convolution_convert_fusion
  11.1 0.1 copy.34
  11.3 33.0 %all_gather.21 = bf16[24,4,512]{0,1,2:T(4,128)(2,1)S(1)} all-gather(bf16[24,4,64]{0,1,2:T(4,128)(2,1)S(1)} %copy.34), channel_id=1, replica_groups=mesh['groups'=2,'row'=8,'head'=2] {'row'}, dimensions={2}, use_global_device_ids=true | all-gather | bytes 110592 | tf_op jit(solution)/shard_map/all_gather | solution.py:65
  44.3 0.3 copy.35
  44.7 1.2 fusion.13
  45.9 0.7 subtract_exponential_fusion.1
  46.6 0.1 copy.32
  46.7 2.2 fusion.28
  48.9 2.2 fusion.7
  51.1 3.4 %multiply_add_fusion = f32[24,4,32,512]{3,2,1,0:T(8,128)S(1)} fusion(f32[24,4,32,512]{3,2,1,0:T(8,128)} %param.30, f32[24,4,512]{2,1,0:T(4,128)S(1)} %copy.36, f32[24,4,32]{2,1,0:T(4,128)S(1)} %copy.33, f32[24,4]{1,0:T(8,128)S(1)} %copy.32), kind=kLoop, calls=%fused_computation.10 | loop fusion | flops 4718592 | bytes 12792192 | tf_op jit(solution)/shard_map/add | solution.py:63
  54.5 2.7 copy-done.1
  57.2 3.1 %fusion.26 = f32[24,4,1,512]{3,2,1,0:T(1,128)S(1)} fusion(f32[24,4,32,512]{3,2,1,0:T(8,128)S(1)} %multiply_add_fusion, f32[24,4,32,1]{2,0,1,3:T(8,128)S(1)} %fusion.7), kind=kOutput, calls=%fused_computation.46 | convolution fusion | flops 18874368 | bytes 6500352 | tf_op jit(solution)/shard_map/shj,shje->she/dot_general | solution.py:68
  60.4 0.7 copy.47
  61.2 0.6 copy.38
  61.8 0.6 dynamic-slice
  63.1 70.0 %all-reduce.7.cloned.1.call-done = f32[24,4,512]{2,0,1:T(8,128)} async-done(((f32[24,4,512]{2,0,1:T(8,128)}), f32[24,4,512]{2,0,1:T(8,128)}) %all-reduce.7.cloned.1.call-update) | async-done | bytes 196624 | tf_op jit(solution)/shard_map/psum | solution.py:71
  133.1 1.0 reduce_sum.55
  134.1 1.1 multiply_reduce_fusion
  135.3 3.8 %convolution_bitcast_fusion = f32[24,4096]{1,0:T(8,128)} fusion(bf16[4,64,4096]{2,1,0:T(8,128)(2,1)S(1)} %copy-done, bf16[4,64,4096]{2,1,0:T(8,128)(2,1)} %param.23, f32[24,4,512]{2,0,1:T(8,128)S(1)} %get-tuple-element.86, s32[]{:T(128)S(6)} %select_n.16, f32[4,64]{1,0:T(4,128)S(1)} %copy-done.6, f32[24,4]{0,1:T(4,128)S(1)} %add_rsqrt_fusion, ...), kind=kOutput, calls=%fused_computation.11 | convolution fusion | flops 101099520 | bytes 4854276 | tf_op jit(solution)/shard_map/shj,hjd->sd/dot_general | solution.py:80
  139.1 90.6 %all-reduce.9.cloned.1.call-done = f32[24,4096]{1,0:T(8,128)} async-done(((f32[24,4096]{1,0:T(8,128)}), f32[24,4096]{1,0:T(8,128)}) %all-reduce.9.cloned.1.call-update) | async-done | bytes 393232 | tf_op jit(solution)/shard_map/psum | solution.py:84
  229.6 1.2 fusion.14
  230.8 8.3 %fusion.50 = (f32[24]{0:T(128)S(1)}, f32[24,1572]{1,0:T(8,128)S(1)}) fusion(bf16[1572,4096]{1,0:T(8,128)(2,1)} %param.29, bf16[24,4096]{1,0:T(8,128)(2,1)S(1)} %get-tuple-element.84, f32[4096]{0:T(1024)S(1)} %copy-done.4, f32[24]{0:T(128)S(1)} %add_rsqrt_fusion.1), kind=kOutput, calls=%fused_computation.74 | convolution fusion | flops 309498688 | bytes 13241920 | tf_op jit(solution)/shard_map/sd,vd->sv/dot_general | solution.py:87
  239.1 0.2 dynamic-update-slice
  239.3 0.2 select_reduce_fusion
  239.6 0.2 dynamic-update-slice.1
  239.8 0.2 dynamic-update-slice.2
  240.0 30.9 %all-reduce.3 = (f32[384]{0:T(512)S(1)}, f32[384]{0:T(512)S(1)}, f32[384]{0:T(512)S(1)}) all-reduce(f32[384]{0:T(512)S(1)} %dynamic-update-slice, f32[384]{0:T(512)S(1)} %dynamic-update-slice.1, f32[384]{0:T(512)S(1)} %dynamic-update-slice.2), channel_id=2, replica_groups=mesh['groups'=2,'row'=8,'head'=2] {'row','head'}, use_global_device_ids=true, to_apply=%add | all-reduce | flops 1152 | bytes 9216
  271.2 0.6 constant_dynamic-slice_fusion.3
  271.9 0.1 reshape.56
  272.0 0.6 while.14
  272.7 0.5 add_subtract_fusion
  (55 shorter events, 1.1 us)
Async XLA Ops:
  7.2 128.1 %copy-start = (bf16[4,64,4096]{2,1,0:T(8,128)(2,1)S(1)}, bf16[4,64,4096]{2,1,0:T(8,128)(2,1)}, u32[]{:S(2)}) copy-start(bf16[4,64,4096]{2,1,0:T(8,128)(2,1)} %param.24) | copy-start | bytes 6291460
  7.2 125.9 %all-reduce.7.cloned.1.call-start = ((), (), s32[]{:S(2)}) async-start(), calls=%async_computation | async-start | bytes 393216 | tf_op jit(solution)/shard_map/psum | solution.py:71
  46.6 7.9 %copy-start.5 = (f32[24,4]{0,1:T(4,128)}, f32[24,4]{0,1:T(4,128)S(1)}, u32[]{:S(2)}) copy-start(f32[24,4]{0,1:T(4,128)S(1)} %get-tuple-element.88) | copy-start | bytes 1156
  54.5 2.7 copy-start.1
  57.2 4.6 %copy-start.8 = (u32[32]{0:T(128)S(1)}, u32[32]{0:T(128)}, u32[]{:S(2)}) copy-start(u32[32]{0:T(128)} %constant.57) | copy-start | bytes 388
  57.2 78.0 %copy-start.2 = (bf16[24,4096]{1,0:T(8,128)(2,1)S(1)}, bf16[24,4096]{1,0:T(8,128)(2,1)}, u32[]{:S(2)}) copy-start(bf16[24,4096]{1,0:T(8,128)(2,1)} %param.18) | copy-start | bytes 589828
  57.2 78.0 %copy-start.3 = (f32[4096]{0:T(1024)S(1)}, f32[4096]{0:T(1024)}, u32[]{:S(2)}) copy-start(f32[4096]{0:T(1024)} %param.19) | copy-start | bytes 49156
  57.2 78.1 %copy-start.6 = (f32[4,64]{1,0:T(4,128)S(1)}, f32[4,64]{1,0:T(4,128)}, u32[]{:S(2)}) copy-start(f32[4,64]{1,0:T(4,128)} %param.27) | copy-start | bytes 3076
  57.2 81.8 %copy-start.7 = (s32[24]{0:T(128)S(1)}, s32[24]{0:T(128)}, u32[]{:S(2)}) copy-start(s32[24]{0:T(128)} %param.33) | copy-start | bytes 292
  57.2 173.6 %copy-start.4 = (f32[4096]{0:T(1024)S(1)}, f32[4096]{0:T(1024)}, u32[]{:S(2)}) copy-start(f32[4096]{0:T(1024)} %param.28) | copy-start | bytes 49156
  61.1 168.5 %all-reduce.9.cloned.1.call-start = ((), (), s32[]{:S(2)}) async-start(), calls=%async_computation.1 | async-start | bytes 786432 | tf_op jit(solution)/shard_map/psum | solution.py:84
Sparse Core Ops, SparseCore 0:
  61.2 71.7 all-reduce.6
  139.2 90.4 all-reduce.8
where the time goes:
time: 281 us; the launch traced here: 280 us
  waiting for transfers between devices  161 us (57%)
  blocking collectives  64 us (23%)
  matrix products  23.4 us (8%)
  between operations  15 us (5%)
  other arithmetic  9.78 us (3%)
  local copies, waits for them, and re-layouts  7.02 us (2%)
    psum x1, waiting for transfers between devices, per_device(): projection = lax.psum(partial_terms, ('row', 'head'))  90.6 us
    psum x1, waiting for transfers between devices, per_device(): readout = lax.psum(partial_readout, 'row')  70 us
    all_gather x1, blocking collectives, per_device(): lax.all_gather(value_part, 'row', axis=2, tiled=True).astype(jnp.float32)  33 us
    unnamed x1, blocking collectives  30.9 us
    dot_general x1, matrix products, per_device(): jnp.einsum('sd,vd->sv', final_feat, w_vocab, preferred_element_type=jnp.f...  8.26 us
    dot_general x3, matrix products, project(): jnp.einsum('sd,hjd->shj', normed_in, weights, preferred_element_type=jnp....  7.03 us
  transfers between devices with their start and end apart: 2, of which 2 were waited for; matrix products, arithmetic and copies ran while one was open for 0% of the time, Pallas kernels for 0%

commit v1 on v0

--- a/solution.py
+++ b/solution.py
@@ -68,7 +68,7 @@
     partial_readout = jnp.einsum(
         "shj,shje->she", queries, memory_out, precision=lax.Precision.HIGHEST
     )
-    readout = lax.psum(partial_readout, "row")
+    readout = jnp.sum(lax.all_gather(partial_readout, "row"), axis=0)
     average = jnp.mean(readout, axis=-1)
     centered_full = readout - average[:, :, None]
     variance = jnp.mean(centered_full * centered_full, axis=-1)

time: 281 us -> 255 us (0.907)
  waiting for transfers between devices: 161 us -> 133 us
    psum x1 -> x0, waiting for transfers between devices: 70 us -> none  [per_device(): readout = lax.psum(partial_readout, 'row')]
    all_gather x0 -> x1, waiting for transfers between devices: none -> 43.5 us  [per_device(): readout = jnp.sum(lax.all_gather(partial_readout, 'row'), axis=0)]
where the time goes in v1:
time: 255 us; the launch traced here: 254 us
  waiting for transfers between devices  133 us (52%)
  blocking collectives  64 us (25%)
  matrix products  23.4 us (9%)
  between operations  15 us (6%)
  other arithmetic  11.3 us (4%)
  local copies, waits for them, and re-layouts  7.08 us (3%)
    psum x1, waiting for transfers between devices, per_device(): projection = lax.psum(partial_terms, ('row', 'head'))  89.9 us
    all_gather x1, waiting for transfers between devices, per_device(): readout = jnp.sum(lax.all_gather(partial_readout, 'row'), axis=0)  43.5 us
    all_gather x1, blocking collectives, per_device(): lax.all_gather(value_part, 'row', axis=2, tiled=True).astype(jnp.float32)  33 us
    unnamed x1, blocking collectives  30.9 us
    dot_general x1, matrix products, per_device(): jnp.einsum('sd,vd->sv', final_feat, w_vocab, preferred_element_type=jnp.f...  8.26 us
    dot_general x3, matrix products, project(): jnp.einsum('sd,hjd->shj', normed_in, weights, preferred_element_type=jnp....  7.03 us
  transfers between devices with their start and end apart: 2, of which 2 were waited for; matrix products, arithmetic and copies ran while one was open for 0% of the time, Pallas kernels for 0%

profile of v1, /device:TPU:0, one launch (start us, length us, event | category | flops | bytes accessed | tf_op | source)
XLA Modules:
  0.0 254.4 jit_solution(5920472809546466707)
XLA Ops:
  7.2 1.2 fusion.17
  8.5 2.7 %convolution_convert_fusion = bf16[24,4,64]{2,0,1:T(8,128)(2,1)S(1)} fusion(bf16[4,64,4096]{2,1,0:T(8,128)(2,1)} %param.22, bf16[24,4096]{1,0:T(8,128)(2,1)} %param.18, f32[4096]{0:T(1024)} %param.19, f32[24]{0:T(128)S(1)} %add_rsqrt_fusion.2), kind=kOutput, calls=%fused_computation.21 | convolution fusion | flops 50731008 | bytes 2322528 | tf_op jit(solution)/shard_map/sd,hjd->shj/dot_general | solution.py:47
  11.1 0.1 copy.56
  11.3 33.0 %all_gather.27 = bf16[24,4,512]{0,1,2:T(4,128)(2,1)S(1)} all-gather(bf16[24,4,64]{0,1,2:T(4,128)(2,1)S(1)} %copy.56), channel_id=1, replica_groups=mesh['groups'=2,'row'=8,'head'=2] {'row'}, dimensions={2}, use_global_device_ids=true | all-gather | bytes 110592 | tf_op jit(solution)/shard_map/all_gather | solution.py:65
  44.3 0.3 copy.57
  44.7 1.2 fusion.13
  45.9 0.7 subtract_exponential_fusion.1
  46.6 0.1 copy.54
  46.7 2.2 fusion.28
  48.9 2.2 fusion.7
  51.1 3.4 %multiply_add_fusion = f32[24,4,32,512]{3,2,1,0:T(8,128)S(1)} fusion(f32[24,4,32,512]{3,2,1,0:T(8,128)} %param.30, f32[24,4,512]{2,1,0:T(4,128)S(1)} %copy.58, f32[24,4,32]{2,1,0:T(4,128)S(1)} %copy.55, f32[24,4]{1,0:T(8,128)S(1)} %copy.54), kind=kLoop, calls=%fused_computation.10 | loop fusion | flops 4718592 | bytes 12792192 | tf_op jit(solution)/shard_map/add | solution.py:63
  54.5 2.7 %copy-done.1 = f32[24,4,32,512]{3,2,1,0:T(8,128)} copy-done((f32[24,4,32,512]{3,2,1,0:T(8,128)}, f32[24,4,32,512]{3,2,1,0:T(8,128)S(1)}, u32[]{:S(2)}) %copy-start.1) | copy-done | bytes 6291480
  57.2 3.1 %fusion.26 = f32[24,4,1,512]{3,2,1,0:T(1,128)S(1)} fusion(f32[24,4,32,512]{3,2,1,0:T(8,128)S(1)} %multiply_add_fusion, f32[24,4,32,1]{2,0,1,3:T(8,128)S(1)} %fusion.7), kind=kOutput, calls=%fused_computation.46 | convolution fusion | flops 18874368 | bytes 6500352 | tf_op jit(solution)/shard_map/shj,shje->she/dot_general | solution.py:68
  60.4 0.7 copy.74
  61.2 0.6 copy.62
  61.8 0.6 dynamic-slice
  63.0 43.5 %all-gather.6.cloned.1.call-done = f32[192,4,512]{2,1,0:T(4,128)} async-done(((f32[24,4,512]{2,1,0:T(4,128)}), f32[192,4,512]{2,1,0:T(4,128)}) %all-gather.6.cloned.1.call-update) | async-done | bytes 1572880 | tf_op jit(solution)/shard_map/all_gather | solution.py:71
  106.6 1.7 reduce.1
  108.4 1.7 reduce_sum.64
  110.1 0.2 multiply_reduce_fusion
  110.3 3.8 %convolution_bitcast_fusion = f32[24,4096]{1,0:T(8,128)} fusion(bf16[4,64,4096]{2,1,0:T(8,128)(2,1)S(1)} %copy-done, bf16[4,64,4096]{2,1,0:T(8,128)(2,1)} %param.23, f32[24,4,512]{2,0,1:T(8,128)S(1)} %get-tuple-element.101, s32[]{:T(128)S(6)} %select_n.16, f32[4,64]{1,0:T(4,128)S(1)} %copy-done.6, f32[24,4]{0,1:T(4,128)S(1)} %add_rsqrt_fusion, ...), kind=kOutput, calls=%fused_computation.11 | convolution fusion | flops 101099520 | bytes 4854276 | tf_op jit(solution)/shard_map/shj,hjd->sd/dot_general | solution.py:80
  114.1 89.9 %all-reduce.6.cloned.1.call-done = f32[24,4096]{1,0:T(8,128)} async-done(((f32[24,4096]{1,0:T(8,128)}), f32[24,4096]{1,0:T(8,128)}) %all-reduce.6.cloned.1.call-update) | async-done | bytes 393232 | tf_op jit(solution)/shard_map/psum | solution.py:84
  204.0 1.2 fusion.14
  205.1 8.3 %fusion.50 = (f32[24]{0:T(128)S(1)}, f32[24,1572]{1,0:T(8,128)S(1)}) fusion(bf16[1572,4096]{1,0:T(8,128)(2,1)} %param.29, bf16[24,4096]{1,0:T(8,128)(2,1)S(1)} %get-tuple-element.99, f32[4096]{0:T(1024)S(1)} %copy-done.4, f32[24]{0:T(128)S(1)} %add_rsqrt_fusion.1), kind=kOutput, calls=%fused_computation.74 | convolution fusion | flops 309498688 | bytes 13241920 | tf_op jit(solution)/shard_map/sd,vd->sv/dot_general | solution.py:87
  213.4 0.2 dynamic-update-slice
  213.7 0.2 select_reduce_fusion
  213.9 0.2 dynamic-update-slice.1
  214.1 0.2 dynamic-update-slice.2
  214.3 30.9 %all-reduce.3 = (f32[384]{0:T(512)S(1)}, f32[384]{0:T(512)S(1)}, f32[384]{0:T(512)S(1)}) all-reduce(f32[384]{0:T(512)S(1)} %dynamic-update-slice, f32[384]{0:T(512)S(1)} %dynamic-update-slice.1, f32[384]{0:T(512)S(1)} %dynamic-update-slice.2), channel_id=3, replica_groups=mesh['groups'=2,'row'=8,'head'=2] {'row','head'}, use_global_device_ids=true, to_apply=%add | all-reduce | flops 1152 | bytes 9216
  245.5 0.6 constant_dynamic-slice_fusion.3
  246.4 0.6 while.14
  247.0 0.5 add_subtract_fusion
  (58 shorter events, 1.3 us)
Async XLA Ops:
  7.2 103.1 %copy-start = (bf16[4,64,4096]{2,1,0:T(8,128)(2,1)S(1)}, bf16[4,64,4096]{2,1,0:T(8,128)(2,1)}, u32[]{:S(2)}) copy-start(bf16[4,64,4096]{2,1,0:T(8,128)(2,1)} %param.24) | copy-start | bytes 6291460
  7.2 99.4 %all-gather.6.cloned.1.call-start = ((), (), s32[]{:S(2)}) async-start(), calls=%async_computation.1 | async-start | bytes 1769472 | tf_op jit(solution)/shard_map/all_gather | solution.py:71
  46.6 7.9 %copy-start.5 = (f32[24,4]{0,1:T(4,128)}, f32[24,4]{0,1:T(4,128)S(1)}, u32[]{:S(2)}) copy-start(f32[24,4]{0,1:T(4,128)S(1)} %get-tuple-element.103) | copy-start | bytes 1156
  54.5 2.7 %copy-start.1 = (f32[24,4,32,512]{3,2,1,0:T(8,128)}, f32[24,4,32,512]{3,2,1,0:T(8,128)S(1)}, u32[]{:S(2)}) copy-start(f32[24,4,32,512]{3,2,1,0:T(8,128)S(1)} %multiply_add_fusion) | copy-start | bytes 18874372
  57.2 4.6 %copy-start.8 = (u32[32]{0:T(128)S(1)}, u32[32]{0:T(128)}, u32[]{:S(2)}) copy-start(u32[32]{0:T(128)} %constant.57) | copy-start | bytes 388
  57.2 53.1 %copy-start.2 = (bf16[24,4096]{1,0:T(8,128)(2,1)S(1)}, bf16[24,4096]{1,0:T(8,128)(2,1)}, u32[]{:S(2)}) copy-start(bf16[24,4096]{1,0:T(8,128)(2,1)} %param.18) | copy-start | bytes 589828
  57.2 53.1 %copy-start.3 = (f32[4096]{0:T(1024)S(1)}, f32[4096]{0:T(1024)}, u32[]{:S(2)}) copy-start(f32[4096]{0:T(1024)} %param.19) | copy-start | bytes 49156
  57.2 53.1 %copy-start.6 = (f32[4,64]{1,0:T(4,128)S(1)}, f32[4,64]{1,0:T(4,128)}, u32[]{:S(2)}) copy-start(f32[4,64]{1,0:T(4,128)} %param.27) | copy-start | bytes 3076
  60.3 53.7 %copy-start.7 = (s32[24]{0:T(128)S(1)}, s32[24]{0:T(128)}, u32[]{:S(2)}) copy-start(s32[24]{0:T(128)} %param.33) | copy-start | bytes 292
  60.3 144.8 %copy-start.4 = (f32[4096]{0:T(1024)S(1)}, f32[4096]{0:T(1024)}, u32[]{:S(2)}) copy-start(f32[4096]{0:T(1024)} %param.28) | copy-start | bytes 49156
  61.1 142.9 %all-reduce.6.cloned.1.call-start = ((), (), s32[]{:S(2)}) async-start(), calls=%async_computation | async-start | bytes 786432 | tf_op jit(solution)/shard_map/psum | solution.py:84
Sparse Core Ops, SparseCore 0:
  61.2 45.2 all-gather.5
  114.2 89.7 all-reduce.5
